TPU v7x, 256 devices: a whole 4x4x8 slice. The times are simulated.
256 devices in a mesh: shadow: 32 (over z, y_lo, core), vocab: 8 (over y_hi, x).
Axes of the slice: x: 4, y: 4 (y_hi: 2, y_lo: 2; y = y_hi * 2 + y_lo), z: 8, core: 2. Of those that a mesh axis runs over, the one named last changes fastest.
Arguments:
- hidden: bfloat16 [128, 128, 2048], P('shadow'), may hold values from -18 to 18
- targets: int32 [128], replicated, may hold values from 0 to 32767
- membership: int32 [128, 4], P('shadow'), may hold values from 0 to 1, as said below
- unembedding: bfloat16 [32768, 2048], P(('shadow', 'vocab')), may hold values from -1 to 1
Outputs:
- score: float32 [128, 128], P('shadow', 'vocab')
Inputs may be any that keep to these rules, and one draw needn't show every extreme that they name: `membership`: each candidate sequence is a member of exactly 64 of the shadow models.
All inputs are finite; a program needn't handle non-finite values.
Results may differ from a plain program's by a relative error of at most 0.00055.
Values may be sent and summed in bfloat16 or wider, within the bound.
A program may use at most 64 MiB of HBM per device.

v0:
```python
import jax
import jax.numpy as jnp
from jax import lax
from jax.sharding import PartitionSpec as P

SEQ = 32


NEG_FILL = -1e30
VAR_FLOOR = 0.5


def copy_for_each(value, axis):
    copies = jnp.broadcast_to(value, (lax.axis_size(axis), *value.shape))
    return lax.all_to_all(copies, axis, split_axis=0, concat_axis=0, tiled=True)


def all_in_one(value, axis):
    leaves = jax.tree.leaves(value)
    sequence = sorted(range(len(leaves)), key=lambda k: -leaves[k].size)
    width = (1, *leaves[sequence[0]].shape)[-1]
    lines = [
        jnp.pad(leaves[k].reshape(-1), (0, -leaves[k].size % width)).reshape(-1, width)
        for k in sequence
    ]
    both, at, found = (copy_for_each(jnp.concatenate(lines), axis), 0, {})
    for k, line in zip(sequence, lines):
        share = both[:, at : at + len(line)].reshape(len(both), -1)
        found[k] = share[:, : leaves[k].size].reshape(-1, *leaves[k].shape)
        at += len(line)
    numbers = iter(range(len(leaves)))
    return jax.tree.map(lambda _: found[next(numbers)], value)


def folded_in_pairs(pieces, combine):
    while len(jax.tree.leaves(pieces)[0]) > 1:
        pieces = jax.vmap(combine)(
            *(jax.tree.map(lambda part: part[side::2], pieces) for side in (0, 1))
        )
    return jax.tree.map(lambda part: part[0], pieces)


def joined_all(value, axis, combine):
    pieces = all_in_one(value, axis)
    return folded_in_pairs(pieces, combine)


def over_copies(value, axis):
    everything = copy_for_each(value, axis)
    return jnp.sum(everything, axis=0)


def packed_total(arrays, axis):
    ends = [0]
    for a in arrays:
        ends.append(ends[-1] + a.size)
    total = over_copies(jnp.concatenate([a.ravel() for a in arrays]), axis)
    return tuple((total[b:e].reshape(a.shape) for a, b, e in zip(arrays, ends, ends[1:])))


def start_state(row_count):
    return (
        jnp.full((row_count,), NEG_FILL, jnp.float32),
        jnp.zeros((row_count,), jnp.float32),
        jnp.zeros((row_count,), jnp.float32),
    )


def fold_block(running, flat_rows, wanted, block_rows, vocab_rows):
    highest, summed, target_logit = running
    logits = lax.dot_general(
        flat_rows, block_rows, (((1,), (1,)), ((), ())), preferred_element_type=jnp.float32
    )
    target_hit = wanted[:, None] == vocab_rows[None, :]
    target_logit = jnp.sum(jnp.where(target_hit, logits, 0.0), axis=1)
    others = jnp.where(target_hit, NEG_FILL, logits)
    raised = jnp.maximum(highest, jnp.max(others, axis=1))
    fresh_terms = jnp.where(target_hit, 0.0, jnp.exp(others - raised[:, None]))
    summed = jnp.sum(fresh_terms, axis=1)
    return (raised, summed, target_logit)


def combine_pairs(earlier, latter):
    raised = jnp.maximum(earlier[0], latter[0])
    summed = earlier[1] * jnp.exp(earlier[0] - raised) + latter[1] * jnp.exp(latter[0] - raised)
    return (raised, summed, earlier[2] + latter[2])


def per_device(hidden, targets, membership, unembedding):
    shadow_count, token_count, model_width = hidden.shape
    head_rows = unembedding.shape[0]
    vocab_count = lax.axis_size("vocab")
    vocab_index = lax.axis_index("vocab")
    shadows_total = shadow_count * lax.axis_size("shadow")
    slice_tokens = token_count // vocab_count
    slice_start = vocab_index * slice_tokens
    flat_rows = hidden.reshape(shadow_count * token_count, model_width)
    wanted = jnp.tile(targets, shadow_count)
    block_rows = lax.all_gather(unembedding, "shadow", axis=0, tiled=True)
    gathered = jnp.arange(block_rows.shape[0], dtype=jnp.int32)
    vocab_rows = (
        gathered // head_rows * vocab_count + vocab_index
    ) * head_rows + gathered % head_rows
    highest, summed, target_logit = fold_block(
        start_state(flat_rows.shape[0]), flat_rows, wanted, block_rows, vocab_rows
    )
    highest, summed, target_logit = joined_all(
        (highest, summed, target_logit), "vocab", combine_pairs
    )
    all_confidence = (target_logit - (highest + jnp.log(summed))).reshape(shadow_count, token_count)
    confidence = lax.dynamic_slice_in_dim(all_confidence, slice_start, slice_tokens, 1)
    member_tokens = jnp.repeat(membership, SEQ, axis=1)
    outside = (1 - lax.dynamic_slice_in_dim(member_tokens, slice_start, slice_tokens, 1)).astype(
        jnp.float32
    )
    weighted = outside * confidence
    first_moment, second_moment = packed_total(
        (jnp.sum(weighted, axis=0), jnp.sum(weighted * confidence, axis=0)), "shadow"
    )
    out_count = shadows_total // 2 - outside
    out_mean = (first_moment[None, :] - weighted) / out_count
    out_variance = (
        second_moment[None, :] - weighted * confidence
    ) / out_count - out_mean * out_mean
    return (confidence - out_mean) * lax.rsqrt(jnp.maximum(out_variance, 0.0) + VAR_FLOOR)


def solution(mesh):
    return jax.shard_map(
        per_device,
        mesh=mesh,
        in_specs=(P("shadow", None, None), P(), P("shadow", None), P(("shadow", "vocab"), None)),
        out_specs=P("shadow", "vocab"),
        check_vma=False,
    )
```

profile of v0, /device:TPU:1, one launch (start us, length us, event | category | flops | bytes accessed | tf_op | source)
XLA Modules:
  0.0 166.2 jit_solution(9505137555500328018)
XLA Ops:
  6.5 0.0 copy-start
  6.5 0.0 all-gather.2.cloned.1.call-start
  6.5 0.7 all-gather.2.cloned.1.call-update
  7.3 0.7 broadcast_bitcast_fusion
  7.9 105.2 %all-gather.2.cloned.1.call-done = bf16[4096,2048]{1,0:T(8,128)(2,1)} async-done(((bf16[128,2048]{1,0:T(8,128)(2,1)}), bf16[4096,2048]{1,0:T(8,128)(2,1)}) %all-gather.2.cloned.1.call-update) | async-done | bytes 16777232 | tf_op jit(solution)/shard_map/all_gather | solution.py:99
  113.1 0.0 copy-done
  113.1 12.0 %fusion.2 = (f32[512]{0:T(512)S(1)}, f32[512,4096]{1,0:T(8,128)S(1)}) fusion(s32[4096]{0:T(1024)S(1)} %fusion.12, s32[512]{0:T(512)S(1)} %broadcast_bitcast_fusion, bf16[512,2048]{1,0:T(8,128)(2,1)S(1)} %bitcast.17, bf16[4096,2048]{1,0:T(8,128)(2,1)} %all-gather.2.cloned.1.call-done), kind=kOutput, calls=%fused_computation.5 | convolution fusion | flops 8596226048 | bytes 27283456 | tf_op jit(solution)/shard_map/dot_general | solution.py:71
  125.1 0.0 copy-start.1
  125.2 3.4 %fusion = (f32[512]{0:T(512)S(1)}, f32[512]{0:T(512)S(1)}) fusion(f32[512,4096]{1,0:T(8,128)S(1)} %get-tuple-element.19, f32[512]{0:T(512)S(1)} %broadcast_maximum_fusion, s32[4096]{0:T(1024)S(1)} %fusion.12, s32[512]{0:T(512)S(1)} %broadcast_bitcast_fusion), kind=kLoop, calls=%fused_computation.3 | loop fusion | flops 14679040 | bytes 8413184 | tf_op jit(solution)/shard_map/reduce_sum | solution.py:79
  128.6 0.6 broadcast_in_dim.28
  129.2 6.4 %all-to-all-start = ((f32[8,3,512]{2,1,0:T(4,128)}), f32[8,3,512]{2,1,0:T(4,128)S(1)}, u32[]{:S(2)}, u32[]{:S(2)}) async-start(f32[8,3,512]{2,1,0:T(4,128)} %broadcast_in_dim.28), calls=%async_computation | async-start | bytes 131072 | tf_op jit(solution)/shard_map/all_to_all | solution.py:15
  135.6 0.0 copy-done.1
  135.7 0.1 broadcast_in_dim.29
  135.7 0.1 reshape.79
  135.8 6.5 %all-to-all-done = f32[8,3,512]{2,1,0:T(4,128)S(1)} async-done(((f32[8,3,512]{2,1,0:T(4,128)}), f32[8,3,512]{2,1,0:T(4,128)S(1)}, u32[]{:S(2)}, u32[]{:S(2)}) %all-to-all-start) | async-done | bytes 49184 | tf_op jit(solution)/shard_map/all_to_all | solution.py:15
  142.8 0.1 fusion.17
  142.9 0.1 pad_maximum_fusion.1
  143.0 15.7 %all_to_all.11 = f32[32,1,32]{2,1,0:T(1,128)S(1)} all-to-all(f32[32,1,32]{2,1,0:T(1,128)S(1)} %broadcast_in_dim.30), channel_id=1, replica_groups=mesh['shadow'=32,'vocab'=8] {'shadow'}, dimensions={0} | all-to-all | bytes 8192 | tf_op jit(solution)/shard_map/all_to_all | solution.py:15
  158.6 0.1 fusion.21
  158.7 0.7 rsqrt_multiply_fusion
  (25 shorter events, 0.5 us)
Async XLA Ops:
  6.5 106.6 %copy-start = (bf16[4,128,2048]{2,1,0:T(8,128)(2,1)S(1)}, bf16[4,128,2048]{2,1,0:T(8,128)(2,1)}, u32[]{:S(2)}) copy-start(bf16[4,128,2048]{2,1,0:T(8,128)(2,1)} %param.4) | copy-start | bytes 6291460
  6.5 106.6 %all-gather.2.cloned.1.call-start = ((), (), s32[]{:S(2)}) async-start(), calls=%async_computation.2 | async-start | bytes 17301504 | tf_op jit(solution)/shard_map/all_gather | solution.py:99
  125.1 10.5 %copy-start.1 = (s32[4,4]{1,0:T(4,128)S(1)}, s32[4,4]{1,0:T(4,128)}, u32[]{:S(2)}) copy-start(s32[4,4]{1,0:T(4,128)} %param.6) | copy-start | bytes 196
  129.2 13.1 %all-to-all-start = ((f32[8,3,512]{2,1,0:T(4,128)}), f32[8,3,512]{2,1,0:T(4,128)S(1)}, u32[]{:S(2)}, u32[]{:S(2)}) async-start(f32[8,3,512]{2,1,0:T(4,128)} %broadcast_in_dim.28), calls=%async_computation | async-start | bytes 131072 | tf_op jit(solution)/shard_map/all_to_all | solution.py:15
Sparse Core Ops, SparseCore 0:
  9.2 103.8 all-gather.1
where the time goes:
time: 166 us
  waiting for transfers between devices  112 us (67%)
  blocking collectives  15.7 us (9%)
  between operations  13.5 us (8%)
  matrix products  12 us (7%)
  starting transfers between devices  6.42 us (4%)
  other arithmetic  4.39 us (3%)
  local copies, waits for them, and re-layouts  1.87 us (1%)
    all_gather x1, waiting for transfers between devices, per_device(): block_rows = lax.all_gather(unembedding, 'shadow', axis=0, tiled=True)  105 us
    all_to_all x1, blocking collectives, copy_for_each(): return lax.all_to_all(copies, axis, split_axis=0, concat_axis=0, tiled=True)  15.7 us
    dot_general x1, matrix products, fold_block(): lax.dot_general(flat_rows, block_rows, (((1,), (1,)), ((), ())), preferre...  12 us
    all_to_all x1, waiting for transfers between devices, copy_for_each(): return lax.all_to_all(copies, axis, split_axis=0, concat_axis=0, tiled=True)  6.54 us
    all_to_all x1, starting transfers between devices, copy_for_each(): return lax.all_to_all(copies, axis, split_axis=0, concat_axis=0, tiled=True)  6.42 us
    reduce_sum x1, other arithmetic, fold_block(): summed = jnp.sum(fresh_terms, axis=1)  3.42 us
  transfers between devices with their start and end apart: 2, of which 2 were waited for; matrix products, arithmetic and copies ran while one was open for 0% of the time, Pallas kernels for 0%

commit v1 on v0

v1 whole, which is shorter than its diff:
```python
import functools

import jax
import jax.numpy as jnp
from jax import lax
from jax.experimental import pallas as pl
from jax.experimental.pallas import tpu as pltpu
from jax.sharding import PartitionSpec as P

SEQ = 32
NEG_FILL = -1e30
VAR_FLOOR = 0.5
MESH = pl.DeviceIdType.MESH
NZ = 8
HALF = 64
NT = 256


def kernel(
    hidden_hbm, head_hbm, targets_ref, member_ref, out_ref,
    hid, head, logits, high, total, hit_logit, tg, msg, got1, msg2, got2,
    local_sem, up_send, up_recv, dn_send, dn_recv, yu_send, yu_recv, yd_send, yd_recv,
    core_send, core_recv, tail_send, tail_recv,
):
    shadow = lax.axis_index("shadow")
    vocab = lax.axis_index("vocab")
    z = shadow // 4
    y_lo = (shadow // 2) % 2
    core = shadow % 2
    y_hi = vocab // 4
    x = vocab % 4
    y = y_hi * 2 + y_lo

    def device(z_, y_, x_, core_):
        return ((z_ * 2 + y_ % 2) * 2 + core_, (y_ // 2) * 4 + x_)

    up = device((z + 1) % NZ, y, x, core)
    down = device((z + NZ - 1) % NZ, y, x, core)
    y_up = device(z, (y + 1) % 4, x, core)
    y_dn = device(z, (y + 3) % 4, x, core)
    partner = device(z, y, x, 1 - core)

    own_head = pltpu.make_async_copy(head_hbm, head.at[0], local_sem.at[0])
    own_hid = pltpu.make_async_copy(hidden_hbm, hid.at[0], local_sem.at[1])
    own_head.start()
    own_hid.start()

    place = (y_lo * 2 + core) * 8 + vocab

    def plane_device(p):
        return (z * 4 + p // 8, p % 8)

    barrier = pltpu.get_barrier_semaphore()

    def greet(k, _):
        pl.semaphore_signal(barrier, inc=1, device_id=plane_device((place + k) % 32), device_id_type=MESH)
        return 0

    pl.semaphore_signal(barrier, inc=1, device_id=up, device_id_type=MESH)
    pl.semaphore_signal(barrier, inc=1, device_id=down, device_id_type=MESH)
    lax.fori_loop(1, 32, greet, 0)

    high[...] = jnp.full_like(high, NEG_FILL)
    total[...] = jnp.zeros_like(total)
    hit_logit[...] = jnp.zeros_like(hit_logit)
    wide = jnp.broadcast_to(targets_ref[...], (8, 128))
    tg[:, 0:128] = wide
    tg[:, 128:256] = wide

    pl.semaphore_wait(barrier, 33)
    own_head.wait()

    def ring_copy(k, upward):
        send, recv = (up_send, up_recv) if upward else (dn_send, dn_recv)
        side = 0 if upward else HALF
        if k < 2:
            half = k if upward else 1 - k
            src = head.at[0, pl.ds(half * HALF, HALF), :]
        else:
            src = head.at[k - 1, pl.ds(side, HALF), :]
        return pltpu.make_async_remote_copy(
            src_ref=src, dst_ref=head.at[k + 1, pl.ds(side, HALF), :],
            send_sem=send.at[k], recv_sem=recv.at[k],
            device_id=up if upward else down, device_id_type=MESH,
        )

    for k in range(2):
        ring_copy(k, True).start()
        ring_copy(k, False).start()

    own_hid.wait()

    def y_copy(i, upward):
        send, recv = (yu_send, yu_recv) if upward else (yd_send, yd_recv)
        rows = pl.ds((0 if upward else 256) + i * 128, 128)
        return pltpu.make_async_remote_copy(
            src_ref=hid.at[0, rows, :], dst_ref=hid.at[2, rows, :],
            send_sem=send.at[i], recv_sem=recv.at[i],
            device_id=y_up if upward else y_dn, device_id_type=MESH,
        )

    def core_copy(i):
        if i == 0:
            src, dst = hid.at[0], hid.at[1]
        else:
            rows = pl.ds([0, 256, 128, 384][i - 1], 128)
            src, dst = hid.at[2, rows, :], hid.at[3, rows, :]
        return pltpu.make_async_remote_copy(
            src_ref=src, dst_ref=dst, send_sem=core_send.at[i], recv_sem=core_recv.at[i],
            device_id=partner, device_id_type=MESH,
        )

    for i in range(2):
        y_copy(i, True).start()
        y_copy(i, False).start()
    core_copy(0).start()

    def base_of(u):
        slot, side = u // 2, u % 2
        if slot == 0:
            zs, half = z, side
        else:
            hops = (slot + 1) // 2
            zs = (z + NZ - hops) % NZ if side == 0 else (z + hops) % NZ
            half = (slot + 1) % 2 if side == 0 else slot % 2
        return (((zs * 2 + y_lo) * 2 + core) * 8 + vocab) * 128 + half * HALF

    def product(slot, count, buf, column):
        piece, row = column // 512, pl.multiple_of(column % 512, NT)
        lhs = head[slot:slot + count].reshape(count * 128, head.shape[2])
        rhs = hid[piece, pl.ds(row, NT), :]
        logits[buf, 0:count * 128] = lax.dot_general(
            lhs, rhs, (((1,), (1,)), ((), ())), preferred_element_type=jnp.float32
        )

    def fold(slot, count, buf, column):
        cols = pl.ds(pl.multiple_of(column, NT), NT)
        ids = lax.broadcasted_iota(jnp.int32, (8, 8, NT), 1) + 8 * lax.broadcasted_iota(
            jnp.int32, (8, 8, NT), 0
        )
        found = jnp.zeros((8, NT), jnp.float32)
        others = []
        old = high[:, cols]
        new = old
        for u in range(2 * count):
            v = logits[buf, u * HALF:(u + 1) * HALF, :].reshape(8, 8, NT)
            hit = (tg[...] - base_of(2 * slot + u))[None] == ids
            found = found + jnp.sum(jnp.where(hit, v, 0.0), axis=0)
            v = jnp.where(hit, 2.0 * NEG_FILL, v)
            new = jnp.maximum(new, jnp.max(v, axis=0))
            others.append(v)
        fresh = total[:, cols] * jnp.exp(old - new)
        for v in others:
            fresh = fresh + jnp.sum(jnp.exp(v - new[None]), axis=0)
        high[:, cols] = new
        total[:, cols] = fresh
        hit_logit[:, cols] = hit_logit[:, cols] + found

    def multiply(slot, count, first, columns):
        tiles = columns // NT
        product(slot, count, 0, first)

        def pair(i, _):
            at = first + i * (2 * NT)
            fold(slot, count, 0, at)
            product(slot, count, 1, at + NT)
            fold(slot, count, 1, at + NT)
            product(slot, count, 0, at + 2 * NT)
            return 0

        lax.fori_loop(0, tiles // 2 - 1, pair, 0)
        last = first + columns - 2 * NT
        fold(slot, count, 0, last)
        product(slot, count, 1, last + NT)
        fold(slot, count, 1, last + NT)

    def arrive(k):
        ring_copy(k, True).wait_recv()
        if k < 5:
            ring_copy(k + 2, True).start()
        ring_copy(k, False).wait_recv()
        if k < 5:
            ring_copy(k + 2, False).start()

    def arrive_y(i):
        y_copy(i, True).wait_recv()
        core_copy(1 + 2 * i).start()
        y_copy(i, False).wait_recv()
        core_copy(2 + 2 * i).start()

    core_copy(0).wait_recv()
    arrive(0)
    multiply(0, 2, 0, 1024)
    arrive(1)
    arrive_y(0)
    arrive(2)
    multiply(2, 2, 0, 1024)
    arrive(3)
    arrive_y(1)
    for i in range(1, 5):
        core_copy(i).wait_recv()
    multiply(0, 2, 1024, 1024)
    multiply(2, 2, 1024, 1024)
    arrive(4)
    multiply(4, 2, 0, 2048)
    arrive(5)
    multiply(6, 1, 0, 2048)
    arrive(6)
    multiply(7, 1, 0, 2048)

    lane = lax.broadcasted_iota(jnp.int32, (8, 128), 1)
    line = lax.broadcasted_iota(jnp.int32, (8, 128), 0)
    peak = jnp.max(high[...], axis=0, keepdims=True)
    summed = jnp.sum(total[...] * jnp.exp(high[...] - peak), axis=0, keepdims=True)
    partial = peak + jnp.log(summed)
    at_target = jnp.sum(hit_logit[...], axis=0, keepdims=True)
    for q in range(4):
        tile = jnp.zeros((8, 128), jnp.float32)
        for j in range(4):
            part = slice(q * 512 + j * 128, q * 512 + (j + 1) * 128)
            tile = jnp.where(line == j, jnp.broadcast_to(partial[:, part], (8, 128)), tile)
            tile = jnp.where(line == 4 + j, jnp.broadcast_to(at_target[:, part], (8, 128)), tile)
        swapped = tile
        for d in range(1, 8):
            moved = pltpu.roll(pltpu.roll(tile, d, 0), 128 - 16 * d, 1)
            swapped = jnp.where((line - lane // 16 + 8) % 8 == d, moved, swapped)
        for r in range(8):
            msg[q * 8 + r] = swapped[r:r + 1, :]

    def to_plane(k, _):
        p = (place + k) % 32
        q = ((y_lo + p // 16) % 2) * 2 + (core + p // 8) % 2
        pltpu.make_async_remote_copy(
            src_ref=msg.at[q * 8 + p % 8], dst_ref=got1.at[31 - k],
            send_sem=tail_send.at[0], recv_sem=tail_recv.at[0],
            device_id=plane_device(p), device_id_type=MESH,
        ).start()
        return 0

    lax.fori_loop(1, 32, to_plane, 0)
    got1[31] = msg[vocab]
    all_plane = pltpu.make_async_remote_copy(
        src_ref=msg.at[0:31], dst_ref=got1.at[0:31],
        send_sem=tail_send.at[0], recv_sem=tail_recv.at[0],
        device_id=partner, device_id_type=MESH,
    )
    all_plane.wait_recv()

    lane = lax.broadcasted_iota(jnp.int32, (1, 128), 1)
    pieces = got1[...]
    top = jnp.max(pieces, axis=0)
    lse = top + jnp.log(jnp.sum(jnp.exp(pieces - top[None]), axis=0))
    target_logit = jnp.sum(pieces, axis=0)
    conf = pltpu.roll(target_logit, 64, 1) - lse
    conf = jnp.where(lane < 64, conf, pltpu.roll(conf, 64, 1))
    group = (lane % 64) // 16
    outside = jnp.zeros((1, 128), jnp.float32)
    for j in range(4):
        free = (1 - member_ref[j, vocab // 2]).astype(jnp.float32)
        outside = jnp.where(group == j, free, outside)
    weighted = outside * conf
    squared = weighted * conf

    def over_groups(value):
        value = value + pltpu.roll(value, 16, 1)
        return value + pltpu.roll(value, 32, 1)

    msg2[...] = jnp.where(lane < 64, over_groups(weighted), over_groups(squared))

    def to_shadows(k, _):
        pltpu.make_async_remote_copy(
            src_ref=msg2, dst_ref=got2.at[31 - k],
            send_sem=tail_send.at[1], recv_sem=tail_recv.at[1],
            device_id=((shadow + k) % 32, vocab), device_id_type=MESH,
        ).start()
        return 0

    lax.fori_loop(1, 32, to_shadows, 0)
    got2[31] = msg2[...]
    all_shadows = pltpu.make_async_remote_copy(
        src_ref=got2.at[0:31], dst_ref=got2.at[0:31],
        send_sem=tail_send.at[1], recv_sem=tail_recv.at[1],
        device_id=partner, device_id_type=MESH,
    )
    all_shadows.wait_recv()
    moments = jnp.sum(got2[...], axis=0)
    swapped = pltpu.roll(moments, 64, 1)
    first = jnp.where(lane < 64, moments, swapped)
    second = jnp.where(lane < 64, swapped, moments)
    count = 64.0 - outside
    mean = (first - weighted) / count
    variance = (second - squared) / count - mean * mean
    score = (conf - mean) * lax.rsqrt(jnp.maximum(variance, 0.0) + VAR_FLOOR)
    rows = jnp.broadcast_to(score, (8, 128))
    placed = rows
    for j in range(1, 4):
        placed = jnp.where(line == j, pltpu.roll(rows, 128 - 16 * j, 1), placed)
    out_ref[...] = placed[0:4, 0:16]

    for k in range(7):
        ring_copy(k, True).wait_send()
        ring_copy(k, False).wait_send()
    for i in range(2):
        y_copy(i, True).wait_send()
        y_copy(i, False).wait_send()
    for i in range(5):
        core_copy(i).wait_send()
    all_plane.wait_send()
    all_shadows.wait_send()


def per_device(hidden, targets, membership, unembedding):
    shadow_count, token_count, width = hidden.shape
    return pl.pallas_call(
        kernel,
        out_shape=jax.ShapeDtypeStruct((4, 16), jnp.float32),
        in_specs=[
            pl.BlockSpec(memory_space=pl.ANY),
            pl.BlockSpec(memory_space=pl.ANY),
            pl.BlockSpec(memory_space=pltpu.VMEM),
            pl.BlockSpec(memory_space=pltpu.SMEM),
        ],
        out_specs=pl.BlockSpec(memory_space=pltpu.VMEM),
        scratch_shapes=[
            pltpu.VMEM((4, 512, width), jnp.bfloat16),
            pltpu.VMEM((8, 128, width), jnp.bfloat16),
            pltpu.VMEM((2, 256, NT), jnp.float32),
            pltpu.VMEM((8, 2048), jnp.float32),
            pltpu.VMEM((8, 2048), jnp.float32),
            pltpu.VMEM((8, 2048), jnp.float32),
            pltpu.VMEM((8, NT), jnp.int32),
            pltpu.VMEM((32, 1, 128), jnp.float32),
            pltpu.VMEM((32, 1, 128), jnp.float32),
            pltpu.VMEM((1, 128), jnp.float32),
            pltpu.VMEM((32, 1, 128), jnp.float32),
            pltpu.SemaphoreType.DMA((2,)),
            pltpu.SemaphoreType.DMA((7,)),
            pltpu.SemaphoreType.DMA((7,)),
            pltpu.SemaphoreType.DMA((7,)),
            pltpu.SemaphoreType.DMA((7,)),
            pltpu.SemaphoreType.DMA((2,)),
            pltpu.SemaphoreType.DMA((2,)),
            pltpu.SemaphoreType.DMA((2,)),
            pltpu.SemaphoreType.DMA((2,)),
            pltpu.SemaphoreType.DMA((5,)),
            pltpu.SemaphoreType.DMA((5,)),
            pltpu.SemaphoreType.DMA((2,)),
            pltpu.SemaphoreType.DMA((2,)),
        ],
        compiler_params=pltpu.CompilerParams(
            collective_id=0, has_side_effects=True, vmem_limit_bytes=48 * 2**20
        ),
        name="score_kernel",
    )(
        hidden.reshape(shadow_count * token_count, width), unembedding,
        targets.reshape(1, token_count), membership,
    )


def solution(mesh):
    return jax.shard_map(
        per_device,
        mesh=mesh,
        in_specs=(P("shadow", None, None), P(), P("shadow", None), P(("shadow", "vocab"), None)),
        out_specs=P("shadow", "vocab"),
        check_vma=False,
    )
```

time: 166 us -> 72 us (0.43)
  waiting for transfers between devices: 112 us -> 0 us
  Pallas kernels: 0 us -> 67.2 us
  blocking collectives: 15.7 us -> 0 us
  between operations: 13.5 us -> 0.01 us
  matrix products: 12 us -> 0 us
  starting transfers between devices: 6.42 us -> 0 us
  other arithmetic: 4.39 us -> 0 us
  local copies, waits for them, and re-layouts: 1.87 us -> 4.55 us
    all_gather x1 -> x0, waiting for transfers between devices: 105 us -> none  [per_device(): block_rows = lax.all_gather(unembedding, 'shadow', axis=0, tiled=True)]
    pallas_call x0 -> x1, Pallas kernels: none -> 67.2 us  [per_device(): pl.pallas_call(kernel, out_shape=jax.ShapeDtypeStruct((4, 16), jnp.float3...]
    all_to_all x1 -> x0, blocking collectives: 15.7 us -> none  [copy_for_each(): return lax.all_to_all(copies, axis, split_axis=0, concat_axis=0, tiled=True)]
    dot_general x1 -> x0, matrix products: 12 us -> none  [fold_block(): lax.dot_general(flat_rows, block_rows, (((1,), (1,)), ((), ())), preferre...]
    all_to_all x1 -> x0, waiting for transfers between devices: 6.54 us -> none  [copy_for_each(): return lax.all_to_all(copies, axis, split_axis=0, concat_axis=0, tiled=True)]
    all_to_all x1 -> x0, starting transfers between devices: 6.42 us -> none  [copy_for_each(): return lax.all_to_all(copies, axis, split_axis=0, concat_axis=0, tiled=True)]
    unnamed x5 -> x9, local copies, waits for them, and re-layouts: 0.01 us -> 4.55 us
    reduce_sum x3 -> x0, other arithmetic: 3.54 us -> none  [the longest x1 3.42 us: fold_block(): summed = jnp.sum(fresh_terms, axis=1)]
  transfers between devices with their start and end apart: 2 -> 0, of which waited for: 2 -> 0; matrix products, arithmetic and copies ran while one was open for 0% -> 0% of each run, Pallas kernels for 0% -> 0%
where the time goes in v1:
time: 72 us; the launch traced here: 71.8 us
  Pallas kernels  67.2 us (93%)
  local copies, waits for them, and re-layouts  4.55 us (6%)
    pallas_call x1, Pallas kernels, per_device(): pl.pallas_call(kernel, out_shape=jax.ShapeDtypeStruct((4, 16), jnp.float3...  67.2 us
    unnamed x9, local copies, waits for them, and re-layouts  4.55 us

profile of v1, /device:TPU:1, one launch (start us, length us, event | category | flops | bytes accessed | tf_op | source)
XLA Modules:
  0.0 71.8 jit_solution(7126764520851541027)
XLA Ops:
  0.0 0.0 copy-start
  0.0 1.6 %copy-done = bf16[4,128,2048]{2,1,0:T(8,128)(2,1)S(1)} copy-done((bf16[4,128,2048]{2,1,0:T(8,128)(2,1)S(1)}, bf16[4,128,2048]{2,1,0:T(8,128)(2,1)}, u32[]{:S(2)}) %copy-start) | copy-done | bytes 2097176
  1.6 0.0 copy-start.1
  1.6 1.0 %copy-done.1 = bf16[128,2048]{1,0:T(8,128)(2,1)S(1)} copy-done((bf16[128,2048]{1,0:T(8,128)(2,1)S(1)}, bf16[128,2048]{1,0:T(8,128)(2,1)}, u32[]{:S(2)}) %copy-start.1) | copy-done | bytes 524312
  2.6 0.0 copy-start.2
  2.6 0.7 copy-done.2
  3.3 0.0 copy-start.3
  3.3 0.7 copy-done.3
  4.0 67.2 %score_kernel.1 = f32[4,16]{1,0:T(4,128)S(1)} custom-call(bf16[512,2048]{1,0:T(8,128)(2,1)S(1)} %bitcast.2, bf16[128,2048]{1,0:T(8,128)(2,1)S(1)} %copy-done.1, s32[1,128]{1,0:T(1,128)S(1)} %bitcast.3, s32[4,4]{1,0:T(4,128)S(1)} %copy-done.2), custom_call_target="tpu_custom_call" | custom-call | tf_op jit(solution)/shard_map/score_kernel/pallas_call | solution.py:314
  71.2 0.6 copy.6
Async XLA Ops:
  0.0 1.6 %copy-start = (bf16[4,128,2048]{2,1,0:T(8,128)(2,1)S(1)}, bf16[4,128,2048]{2,1,0:T(8,128)(2,1)}, u32[]{:S(2)}) copy-start(bf16[4,128,2048]{2,1,0:T(8,128)(2,1)} %param.4) | copy-start | bytes 6291460
  1.6 1.0 %copy-start.1 = (bf16[128,2048]{1,0:T(8,128)(2,1)S(1)}, bf16[128,2048]{1,0:T(8,128)(2,1)}, u32[]{:S(2)}) copy-start(bf16[128,2048]{1,0:T(8,128)(2,1)} %head_hbm.1) | copy-start | bytes 1572868
  2.6 0.7 copy-start.2
  3.3 0.7 copy-start.3

commit v2 on v0

v2 whole, which is shorter than its diff:
```python
import functools

import jax
import jax.numpy as jnp
from jax import lax
from jax.experimental import pallas as pl
from jax.experimental.pallas import tpu as pltpu
from jax.sharding import PartitionSpec as P

NEG_FILL = -1e30
VAR_FLOOR = 0.5
MESH = pl.DeviceIdType.MESH
NZ = 8
HALF = 64
NT = 256
PARTS = 4
ROWS = 64 // PARTS
CUTS = 2
CUT = HALF // CUTS
FIRST_X = (1, 3, 2)

GROUPS = (
    ((0, 0, 0), (0, 0, 1)),
    ((0, -1, 0), (0, 1, 1)),
    ((-1, 0, 0), (1, 0, 1)),
    ((-1, -1, 0), (1, 1, 1)),
    ((-1, 0, 1), (1, 0, 0)),
    ((1, -1, 0), (-1, 1, 1)),
    ((-2, 0, 0), (2, 0, 1)),
    ((-2, -1, 0), (2, 1, 1)),
)


def kernel(
    hidden_hbm, head_hbm, targets_hbm, member_hbm, out_ref,
    targets_ref, member_ref, bases, hid, head, logits, high, total, hit_logit, tg,
    msg, got1, msg2, got2,
    local_sem, z_send, z_recv, y_send, y_recv, c_send, c_recv,
    hz_send, hz_recv, hy_send, hy_recv, hx_send, hx_recv, tail_send, tail_recv,
):
    shadow = lax.axis_index("shadow")
    vocab = lax.axis_index("vocab")
    z = shadow // 4
    y_lo = (shadow // 2) % 2
    core = shadow % 2
    y_hi = vocab // 4
    x = vocab % 4
    y = y_hi * 2 + y_lo

    def device(dz, dy, dx, dcore):
        to_y = (y + dy) % 4
        return (
            (((z + dz) % NZ) * 2 + to_y % 2) * 2 + (core + dcore) % 2,
            (to_y // 2) * 4 + (x + dx) % 4,
        )

    own_head = pltpu.make_async_copy(head_hbm, head.at[pl.ds(0, 2)], local_sem.at[0])
    own_hid = pltpu.make_async_copy(hidden_hbm, hid.at[0], local_sem.at[1])
    own_tg = pltpu.make_async_copy(targets_hbm, targets_ref, local_sem.at[2])
    own_member = pltpu.make_async_copy(member_hbm, member_ref, local_sem.at[3])
    own_head.start()
    own_hid.start()
    own_tg.start()
    own_member.start()

    barrier = pltpu.get_barrier_semaphore()
    near = ((1, 0, 0, 0), (7, 0, 0, 0), (4, 0, 0, 0), (0, 1, 0, 0), (0, 3, 0, 0), (0, 2, 0, 0), (0, 0, 1, 0), (0, 0, 3, 0), (0, 0, 2, 0), (0, 0, 0, 1))
    for offset in near:
        pl.semaphore_signal(barrier, inc=1, device_id=device(*offset), device_id_type=MESH)

    high[...] = jnp.full_like(high, NEG_FILL)
    total[...] = jnp.zeros_like(total)
    hit_logit[...] = jnp.zeros_like(hit_logit)
    for g in range(8):
        for u in range(4):
            dz, dy, half = GROUPS[g][u % 2]
            at_y = (y + dy + 4) % 4
            block = ((((z + dz + NZ) % NZ) * 2 + at_y % 2) * 2 + (core + u // 2) % 2) * 8 + (at_y // 2) * 4 + x
            bases[4 * g + u] = block * (2 * HALF) + half * HALF
    own_tg.wait()
    own_member.wait()
    wide = jnp.broadcast_to(targets_ref[...], (8, 128))
    tg[:, 0:128] = wide
    tg[:, 128:256] = wide

    def z_copy(k, upward, n):
        rows = pl.ds(n * CUT, CUT)
        side = 0 if upward else 1
        src = (side, 1 - side, 8 + side)[k]
        dst = (8, 16, 24)[k] + side
        return pltpu.make_async_remote_copy(
            src_ref=head.at[src, rows, :], dst_ref=head.at[dst, rows, :],
            send_sem=z_send.at[side, k, n], recv_sem=z_recv.at[side, k, n],
            device_id=device(1 if upward else NZ - 1, 0, 0, 0), device_id_type=MESH,
        )

    def y_copy(m, upward, n):
        rows = pl.ds(n * CUT, CUT)
        side = 0 if upward else 1
        src = ((0, 8, 17, 24) if upward else (1, 9, 16, 25))[m]
        return pltpu.make_async_remote_copy(
            src_ref=head.at[src, rows, :], dst_ref=head.at[8 * m + 4 + side, rows, :],
            send_sem=y_send.at[side, m, n], recv_sem=y_recv.at[side, m, n],
            device_id=device(0, 1 if upward else 3, 0, 0), device_id_type=MESH,
        )

    def c_copy(g, side, n):
        rows = pl.ds(n * CUT, CUT)
        return pltpu.make_async_remote_copy(
            src_ref=head.at[4 * g + side, rows, :], dst_ref=head.at[4 * g + 2 + side, rows, :],
            send_sem=c_send.at[side, g, n], recv_sem=c_recv.at[side, g, n],
            device_id=device(0, 0, 0, 1), device_id_type=MESH,
        )

    def hz_copy(i):
        rows = pl.ds(pl.multiple_of(vocab * 64 + i * ROWS, ROWS), ROWS)
        return pltpu.make_async_remote_copy(
            src_ref=hid.at[0, rows, :], dst_ref=hid.at[1, rows, :],
            send_sem=hz_send.at[i], recv_sem=hz_recv.at[i],
            device_id=device(4, 0, 0, 0), device_id_type=MESH,
        )

    def hy_copy(i):
        rows = pl.ds(pl.multiple_of(vocab * 64 + i * ROWS, ROWS), ROWS)
        return pltpu.make_async_remote_copy(
            src_ref=hid.at[1, rows, :], dst_ref=hid.at[1, rows, :],
            send_sem=hy_send.at[i], recv_sem=hy_recv.at[i],
            device_id=device(0, 2, 0, 0), device_id_type=MESH,
        )

    def hx_copy(part, i, dx):
        owner = x
        to_x = dx
        if len(FIRST_X) == 2 and dx == 2:
            to_x = 1 if i % 2 == 0 else 3
            owner = (x + 4 - to_x) % 4
        share = ((y_hi + part) % 2) * 4 + owner
        rows = pl.ds(pl.multiple_of(share * 64 + i * ROWS, ROWS), ROWS)
        return pltpu.make_async_remote_copy(
            src_ref=hid.at[1, rows, :], dst_ref=hid.at[1, rows, :],
            send_sem=hx_send.at[part, i, dx - 1], recv_sem=hx_recv.at[part, i, dx - 1],
            device_id=device(0, 0, to_x, 0), device_id_type=MESH,
        )

    def product(g, piece, tile):
        lhs = head[pl.ds(4 * g, 4)].reshape(4 * HALF, head.shape[2])
        rhs = hid[piece, tile * NT:(tile + 1) * NT, :]
        logits[tile] = lax.dot_general(
            lhs, rhs, (((1,), (1,)), ((), ())), preferred_element_type=jnp.float32
        )

    def fold(g, piece, tile):
        cols = slice(tile * NT, (tile + 1) * NT)
        ids = lax.broadcasted_iota(jnp.int32, (8, 8, NT), 1) + 8 * lax.broadcasted_iota(
            jnp.int32, (8, 8, NT), 0
        )
        found = hit_logit[piece, :, cols]
        others = []
        old = high[piece, :, cols]
        new = old
        for u in range(4):
            v = logits[tile, u * HALF:(u + 1) * HALF, :].reshape(8, 8, NT)
            hit = (tg[...] - bases[4 * g + u])[None] == ids
            found = found + jnp.sum(jnp.where(hit, v, 0.0), axis=0)
            v = jnp.where(hit, 2.0 * NEG_FILL, v)
            new = jnp.maximum(new, jnp.max(v, axis=0))
            others.append(v)
        fresh = total[piece, :, cols] * jnp.exp(old - new)
        for v in others:
            fresh = fresh + jnp.sum(jnp.exp(v - new[None]), axis=0)
        high[piece, :, cols] = new
        total[piece, :, cols] = fresh
        hit_logit[piece, :, cols] = found

    def multiply(g, piece):
        product(g, piece, 0)
        product(g, piece, 1)
        fold(g, piece, 0)
        fold(g, piece, 1)

    def multiply_many(first, last, piece):
        def step(g, _):
            multiply(g, piece)
            return 0

        lax.fori_loop(first, last, step, 0)

    def on_z(k, n):
        z_copy(k, True, n).wait_recv()
        if k == 0:
            z_copy(2, True, n).start()
        y_copy(k + 1, k != 1, n).start()
        c_copy(2 * k + 2, 0, n).start()
        z_copy(k, False, n).wait_recv()
        if k == 0:
            z_copy(2, False, n).start()
        y_copy(k + 1, k == 1, n).start()
        c_copy(2 * k + 2, 1, n).start()

    def on_y(m, n):
        for side in range(2):
            y_copy(m, side == 0, n).wait_recv()
            c_copy(2 * m + 1, side, n).start()

    def on_c(g):
        for side in range(2):
            for n in range(CUTS):
                c_copy(g, side, n).wait_recv()

    def on_hz(i):
        hz_copy(i).wait_recv()
        hy_copy(i).start()
        for dx in FIRST_X:
            hx_copy(0, i, dx).start()

    def on_hy(i):
        hy_copy(i).wait_recv()
        for dx in FIRST_X:
            hx_copy(1, i, dx).start()

    def on_hx(part, i):
        hx_copy(part, i, 1).wait_recv()
        if i % 2 == 0:
            hx_copy(part, i, 2).start()
        hx_copy(part, i, 3).wait_recv()
        if i % 2 == 1:
            hx_copy(part, i, 2).start()

    def on_hend(first_piece, last_piece):
        for part in range(2):
            for i in range(first_piece, last_piece):
                if len(FIRST_X) == 3:
                    hx_copy(part, i, 1).wait_recv()
                    hx_copy(part, i, 3).wait_recv()
                hx_copy(part, i, 2).wait_recv()

    pl.semaphore_wait(barrier, len(near))
    own_head.wait()
    for n in range(CUTS):
        c_copy(0, 0, n).start()
        c_copy(0, 1, n).start()
    for n in range(CUTS):
        y_copy(0, True, n).start()
        y_copy(0, False, n).start()
    own_hid.wait()
    hz_copy(0).start()
    hz_copy(1).start()
    hz_copy(2).start()
    hz_copy(3).start()
    z_copy(0, True, 0).start()
    z_copy(0, False, 0).start()
    z_copy(0, True, 1).start()
    z_copy(0, False, 1).start()
    z_copy(1, True, 0).start()
    z_copy(1, False, 0).start()
    z_copy(1, True, 1).start()
    z_copy(1, False, 1).start()
    on_c(0)
    multiply(0, 0)
    on_y(0, 0)
    on_hz(0)
    on_y(0, 1)
    on_c(1)
    multiply(1, 0)
    on_hz(1)
    on_hy(0)
    on_hz(2)
    on_hy(1)
    on_hz(3)
    on_z(0, 0)
    on_hy(2)
    on_z(0, 1)
    on_hy(3)
    on_c(2)
    multiply(2, 0)
    on_y(1, 0)
    on_z(1, 0)
    on_y(1, 1)
    on_z(1, 1)
    on_c(3)
    multiply(3, 0)
    on_c(4)
    multiply(4, 0)
    on_y(2, 0)
    on_z(2, 0)
    on_y(2, 1)
    on_z(2, 1)
    on_c(5)
    multiply(5, 0)
    on_c(6)
    multiply(6, 0)
    on_y(3, 0)
    on_hend(0, 4)
    multiply(0, 1)
    multiply(1, 1)
    multiply(2, 1)
    multiply(3, 1)
    on_y(3, 1)
    multiply(4, 1)
    multiply(5, 1)
    multiply(6, 1)
    on_c(7)
    multiply(7, 0)
    multiply(7, 1)

    lane = lax.broadcasted_iota(jnp.int32, (8, 128), 1)
    line = lax.broadcasted_iota(jnp.int32, (8, 128), 0)
    lse_tile = jnp.zeros((8, 128), jnp.float32)
    target_tile = jnp.zeros((8, 128), jnp.float32)
    for piece in range(2):
        peak = jnp.max(high[piece], axis=0, keepdims=True)
        summed = jnp.sum(total[piece] * jnp.exp(high[piece] - peak), axis=0, keepdims=True)
        partial = peak + jnp.log(summed)
        at_target = jnp.sum(hit_logit[piece], axis=0, keepdims=True)
        for j in range(4):
            part = slice(j * 128, (j + 1) * 128)
            here = line == piece * 4 + j
            lse_tile = jnp.where(here, jnp.broadcast_to(partial[:, part], (8, 128)), lse_tile)
            target_tile = jnp.where(here, jnp.broadcast_to(at_target[:, part], (8, 128)), target_tile)

    def swap_groups(tile):
        swapped = tile
        for d in range(1, 8):
            moved = pltpu.roll(pltpu.roll(tile, d, 0), 128 - 16 * d, 1)
            swapped = jnp.where((line - lane // 16 + 8) % 8 == d, moved, swapped)
        return swapped

    lse_tile = swap_groups(lse_tile)
    target_tile = swap_groups(target_tile)
    for r in range(8):
        msg[r, 0] = lse_tile[r:r + 1, :]
        msg[r, 1] = target_tile[r:r + 1, :]

    def to_plane(k, _):
        to = (vocab + k) % 8
        pltpu.make_async_remote_copy(
            src_ref=msg.at[to], dst_ref=got1.at[7 - k],
            send_sem=tail_send.at[0], recv_sem=tail_recv.at[0],
            device_id=(shadow, to), device_id_type=MESH,
        ).start()
        return 0

    lax.fori_loop(1, 8, to_plane, 0)
    got1[7] = msg[vocab]
    all_plane = pltpu.make_async_remote_copy(
        src_ref=msg.at[0:7], dst_ref=got1.at[0:7],
        send_sem=tail_send.at[0], recv_sem=tail_recv.at[0],
        device_id=device(0, 0, 0, 1), device_id_type=MESH,
    )
    lane = lax.broadcasted_iota(jnp.int32, (1, 128), 1)
    group = (lane % 64) // 16
    outside = jnp.zeros((1, 128), jnp.float32)
    for j in range(4):
        free = (1 - member_ref[j, vocab // 2]).astype(jnp.float32)
        outside = jnp.where(group == j, free, outside)
    msg2[2] = outside
    all_plane.wait_recv()

    pieces = got1[:, 0]
    top = jnp.max(pieces, axis=0)
    msg2[0] = top + jnp.log(jnp.sum(jnp.exp(pieces - top[None]), axis=0))
    msg2[1] = jnp.sum(got1[:, 1], axis=0)

    def to_shadows(k, _):
        dz, dy, dcore = k // 4, (k // 2) % 2, k % 2
        to = (((z + dz) % NZ) * 2 + (y_lo + dy) % 2) * 2 + (core + dcore) % 2
        pltpu.make_async_remote_copy(
            src_ref=msg2, dst_ref=got2.at[((NZ - dz) % NZ) * 4 + k % 4],
            send_sem=tail_send.at[1], recv_sem=tail_recv.at[1],
            device_id=(to, vocab), device_id_type=MESH,
        ).start()
        return 0

    lax.fori_loop(1, 32, to_shadows, 0)
    got2[0] = msg2[...]
    all_shadows = pltpu.make_async_remote_copy(
        src_ref=got2.at[1:32], dst_ref=got2.at[1:32],
        send_sem=tail_send.at[1], recv_sem=tail_recv.at[1],
        device_id=device(0, 0, 0, 1), device_id_type=MESH,
    )
    all_shadows.wait_recv()

    def both_planes(row):
        there = jnp.concatenate([got2[16:32, row], got2[0:16, row]], axis=0)
        return got2[:, row], pltpu.roll(there, 64, 2)

    here, there = both_planes(0)
    top = jnp.maximum(here, there)
    lse = top + jnp.log(jnp.exp(here - top) + jnp.exp(there - top))
    here, there = both_planes(1)
    conf = (here + there) - lse
    weighted = jnp.where(lane < 64, got2[:, 2] * conf, 0.0)
    squared = weighted * conf

    def over_groups(value):
        value = jnp.sum(value, axis=0)
        value = value + pltpu.roll(value, 64, 1)
        value = value + pltpu.roll(value, 16, 1)
        return value + pltpu.roll(value, 32, 1)

    first = over_groups(weighted)
    second = over_groups(squared)
    count = 64.0 - outside
    mean = (first - weighted[0]) / count
    variance = (second - squared[0]) / count - mean * mean
    score = (conf[0] - mean) * lax.rsqrt(jnp.maximum(variance, 0.0) + VAR_FLOOR)
    rows = jnp.broadcast_to(score, (8, 128))
    placed = rows
    for j in range(1, 4):
        placed = jnp.where(line == j, pltpu.roll(rows, 128 - 16 * j, 1), placed)
    out_ref[...] = placed[0:4, 0:16]

    for side in range(2):
        for k in range(3):
            for n in range(CUTS):
                z_copy(k, side == 0, n).wait_send()
        for m in range(4):
            for n in range(CUTS):
                y_copy(m, side == 0, n).wait_send()
        for g in range(8):
            for n in range(CUTS):
                c_copy(g, side, n).wait_send()
    for i in range(PARTS):
        hz_copy(i).wait_send()
        hy_copy(i).wait_send()
        for part in range(2):
            for dx in (1, 3, 2):
                hx_copy(part, i, dx).wait_send()
    all_plane.wait_send()
    all_shadows.wait_send()


def per_device(hidden, targets, membership, unembedding):
    shadow_count, token_count, width = hidden.shape
    dma = pltpu.SemaphoreType.DMA
    return pl.pallas_call(
        kernel,
        out_shape=jax.ShapeDtypeStruct((4, 16), jnp.float32),
        in_specs=[pl.BlockSpec(memory_space=pltpu.HBM)] * 4,
        out_specs=pl.BlockSpec(memory_space=pltpu.VMEM),
        scratch_shapes=[
            pltpu.VMEM((1, 128), jnp.int32),
            pltpu.SMEM((4, 4), jnp.int32),
            pltpu.SMEM((32,), jnp.int32),
            pltpu.VMEM((2, 512, width), jnp.bfloat16),
            pltpu.VMEM((32, HALF, width), jnp.bfloat16),
            pltpu.VMEM((2, 4 * HALF, NT), jnp.float32),
            pltpu.VMEM((2, 8, 512), jnp.float32),
            pltpu.VMEM((2, 8, 512), jnp.float32),
            pltpu.VMEM((2, 8, 512), jnp.float32),
            pltpu.VMEM((8, NT), jnp.int32),
            pltpu.VMEM((8, 2, 1, 128), jnp.float32),
            pltpu.VMEM((8, 2, 1, 128), jnp.float32),
            pltpu.VMEM((3, 1, 128), jnp.float32),
            pltpu.VMEM((32, 3, 1, 128), jnp.float32),
            dma((4,)), dma((2, 3, CUTS)), dma((2, 3, CUTS)), dma((2, 4, CUTS)), dma((2, 4, CUTS)),
            dma((2, 8, CUTS)), dma((2, 8, CUTS)),
            dma((PARTS,)), dma((PARTS,)), dma((PARTS,)), dma((PARTS,)),
            dma((2, PARTS, 3)), dma((2, PARTS, 3)), dma((2,)), dma((2,)),
        ],
        compiler_params=pltpu.CompilerParams(
            collective_id=0, has_side_effects=True, vmem_limit_bytes=67043328
        ),
        name="score_kernel",
    )(
        hidden.reshape(shadow_count * token_count, width),
        unembedding.reshape(2, HALF, width),
        targets.reshape(1, token_count), membership,
    )


def solution(mesh):
    return jax.shard_map(
        per_device,
        mesh=mesh,
        in_specs=(P("shadow", None, None), P(), P("shadow", None), P(("shadow", "vocab"), None)),
        out_specs=P("shadow", "vocab"),
        check_vma=False,
    )
```

time: 166 us -> 65.2 us (0.39)
  waiting for transfers between devices: 112 us -> 0 us
  Pallas kernels: 0 us -> 63.8 us
  blocking collectives: 15.7 us -> 0 us
  between operations: 13.5 us -> 0.01 us
  matrix products: 12 us -> 0 us
  starting transfers between devices: 6.42 us -> 0 us
  other arithmetic: 4.39 us -> 0 us
    all_gather x1 -> x0, waiting for transfers between devices: 105 us -> none  [per_device(): block_rows = lax.all_gather(unembedding, 'shadow', axis=0, tiled=True)]
    pallas_call x0 -> x1, Pallas kernels: none -> 63.8 us  [per_device(): pl.pallas_call(kernel, out_shape=jax.ShapeDtypeStruct((4, 16), jnp.float3...]
    all_to_all x1 -> x0, blocking collectives: 15.7 us -> none  [copy_for_each(): return lax.all_to_all(copies, axis, split_axis=0, concat_axis=0, tiled=True)]
    dot_general x1 -> x0, matrix products: 12 us -> none  [fold_block(): lax.dot_general(flat_rows, block_rows, (((1,), (1,)), ((), ())), preferre...]
    all_to_all x1 -> x0, waiting for transfers between devices: 6.54 us -> none  [copy_for_each(): return lax.all_to_all(copies, axis, split_axis=0, concat_axis=0, tiled=True)]
    all_to_all x1 -> x0, starting transfers between devices: 6.42 us -> none  [copy_for_each(): return lax.all_to_all(copies, axis, split_axis=0, concat_axis=0, tiled=True)]
    reduce_sum x3 -> x0, other arithmetic: 3.54 us -> none  [the longest x1 3.42 us: fold_block(): summed = jnp.sum(fresh_terms, axis=1)]
  transfers between devices with their start and end apart: 2 -> 0, of which waited for: 2 -> 0; matrix products, arithmetic and copies ran while one was open for 0% -> 0% of each run, Pallas kernels for 0% -> 0%
where the time goes in v2:
time: 65.2 us; the launch traced here: 65.1 us
  Pallas kernels  63.8 us (98%)
  local copies, waits for them, and re-layouts  1.26 us (2%)
    pallas_call x1, Pallas kernels, per_device(): pl.pallas_call(kernel, out_shape=jax.ShapeDtypeStruct((4, 16), jnp.float3...  63.8 us

profile of v2, /device:TPU:1, one launch (start us, length us, event | category | flops | bytes accessed | tf_op | source)
XLA Modules:
  0.0 65.1 jit_solution(7998788581131199448)
XLA Ops:
  0.0 63.8 %score_kernel.1 = f32[4,16]{1,0:T(4,128)} custom-call(bf16[512,2048]{1,0:T(8,128)(2,1)} %bitcast.3, bf16[2,64,2048]{2,1,0:T(8,128)(2,1)} %bitcast.4, s32[1,128]{1,0:T(1,128)} %bitcast.5, s32[4,4]{1,0:T(4,128)} %member_hbm.1), custom_call_target="tpu_custom_call" | custom-call | tf_op jit(solution)/shard_map/score_kernel/pallas_call | solution.py:436
  63.8 1.3 %copy.6 = f32[4,16]{1,0:T(4,128)} copy(f32[4,16]{1,0:T(4,128)} %score_kernel.1) | data formatting | bytes 512

commit v3 on v2

--- a/solution.py
+++ b/solution.py
@@ -17,6 +17,7 @@
 ROWS = 64 // PARTS
 CUTS = 2
 CUT = HALF // CUTS
+VIA_Z = (1,)
 FIRST_X = (1, 3, 2)
 
 GROUPS = (
@@ -86,8 +87,8 @@
     def z_copy(k, upward, n):
         rows = pl.ds(n * CUT, CUT)
         side = 0 if upward else 1
-        src = (side, 1 - side, 8 + side)[k]
-        dst = (8, 16, 24)[k] + side
+        src = (side, 1 - side, 8 + side, 12 + side)[k]
+        dst = (8, 16, 24, 28)[k] + side
         return pltpu.make_async_remote_copy(
             src_ref=head.at[src, rows, :], dst_ref=head.at[dst, rows, :],
             send_sem=z_send.at[side, k, n], recv_sem=z_recv.at[side, k, n],
@@ -129,28 +130,29 @@
         )
 
     def hx_copy(part, i, dx):
-        owner = x
-        to_x = dx
-        if len(FIRST_X) == 2 and dx == 2:
-            to_x = 1 if i % 2 == 0 else 3
-            owner = (x + 4 - to_x) % 4
-        share = ((y_hi + part) % 2) * 4 + owner
+        share = ((y_hi + part) % 2) * 4 + x
         rows = pl.ds(pl.multiple_of(share * 64 + i * ROWS, ROWS), ROWS)
         return pltpu.make_async_remote_copy(
             src_ref=hid.at[1, rows, :], dst_ref=hid.at[1, rows, :],
             send_sem=hx_send.at[part, i, dx - 1], recv_sem=hx_recv.at[part, i, dx - 1],
-            device_id=device(0, 0, to_x, 0), device_id_type=MESH,
-        )
-
-    def product(g, piece, tile):
-        lhs = head[pl.ds(4 * g, 4)].reshape(4 * HALF, head.shape[2])
-        rhs = hid[piece, tile * NT:(tile + 1) * NT, :]
-        logits[tile] = lax.dot_general(
+            device_id=device(0, 0, dx, 0), device_id_type=MESH,
+        )
+
+    def columns(tile):
+        return pl.ds(pl.multiple_of(tile * NT, NT), NT)
+
+    def product(g, count, piece, tile, buf):
+        lhs = head[4 * g:4 * (g + count)].reshape(4 * count * HALF, head.shape[2])
+        rhs = hid[piece, columns(tile), :]
+        logits[buf, 0:4 * count * HALF] = lax.dot_general(
             lhs, rhs, (((1,), (1,)), ((), ())), preferred_element_type=jnp.float32
         )
 
-    def fold(g, piece, tile):
-        cols = slice(tile * NT, (tile + 1) * NT)
+    def fold(first, count, piece, tile, buf):
+        for g in range(first, first + count):
+            fold_group(g, (g - first) * 4, piece, columns(tile), buf)
+
+    def fold_group(g, at, piece, cols, buf):
         ids = lax.broadcasted_iota(jnp.int32, (8, 8, NT), 1) + 8 * lax.broadcasted_iota(
             jnp.int32, (8, 8, NT), 0
         )
@@ -159,7 +161,7 @@
         old = high[piece, :, cols]
         new = old
         for u in range(4):
-            v = logits[tile, u * HALF:(u + 1) * HALF, :].reshape(8, 8, NT)
+            v = logits[buf, (at + u) * HALF:(at + u + 1) * HALF, :].reshape(8, 8, NT)
             hit = (tg[...] - bases[4 * g + u])[None] == ids
             found = found + jnp.sum(jnp.where(hit, v, 0.0), axis=0)
             v = jnp.where(hit, 2.0 * NEG_FILL, v)
@@ -172,34 +174,30 @@
         total[piece, :, cols] = fresh
         hit_logit[piece, :, cols] = found
 
-    def multiply(g, piece):
-        product(g, piece, 0)
-        product(g, piece, 1)
-        fold(g, piece, 0)
-        fold(g, piece, 1)
-
-    def multiply_many(first, last, piece):
-        def step(g, _):
-            multiply(g, piece)
-            return 0
-
-        lax.fori_loop(first, last, step, 0)
+    def multiply(*tiles):
+        for i, tile in enumerate(tiles):
+            product(*tile, i % 4)
+            if i:
+                fold(*tiles[i - 1], (i - 1) % 4)
+        fold(*tiles[-1], (len(tiles) - 1) % 4)
+
+    own_tile, far_tile = y_hi, 1 - y_hi
 
     def on_z(k, n):
-        z_copy(k, True, n).wait_recv()
-        if k == 0:
-            z_copy(2, True, n).start()
-        y_copy(k + 1, k != 1, n).start()
-        c_copy(2 * k + 2, 0, n).start()
-        z_copy(k, False, n).wait_recv()
-        if k == 0:
-            z_copy(2, False, n).start()
-        y_copy(k + 1, k == 1, n).start()
-        c_copy(2 * k + 2, 1, n).start()
+        for side in range(2):
+            upward = side == 0
+            z_copy(k, upward, n).wait_recv()
+            if k == 0:
+                z_copy(2, upward, n).start()
+            if k < 2 or (k == 2 and n not in VIA_Z):
+                y_copy(k + 1, upward == (k != 1), n).start()
+            c_copy(7 if k == 3 else 2 * k + 2, side, n).start()
 
     def on_y(m, n):
         for side in range(2):
             y_copy(m, side == 0, n).wait_recv()
+            if m == 1 and n in VIA_Z:
+                z_copy(3, side == 0, n).start()
             c_copy(2 * m + 1, side, n).start()
 
     def on_c(g):
@@ -218,21 +216,10 @@
         for dx in FIRST_X:
             hx_copy(1, i, dx).start()
 
-    def on_hx(part, i):
-        hx_copy(part, i, 1).wait_recv()
-        if i % 2 == 0:
-            hx_copy(part, i, 2).start()
-        hx_copy(part, i, 3).wait_recv()
-        if i % 2 == 1:
-            hx_copy(part, i, 2).start()
-
-    def on_hend(first_piece, last_piece):
-        for part in range(2):
-            for i in range(first_piece, last_piece):
-                if len(FIRST_X) == 3:
-                    hx_copy(part, i, 1).wait_recv()
-                    hx_copy(part, i, 3).wait_recv()
-                hx_copy(part, i, 2).wait_recv()
+    def on_hend(part):
+        for i in range(PARTS):
+            for dx in (1, 3, 2):
+                hx_copy(part, i, dx).wait_recv()
 
     pl.semaphore_wait(barrier, len(near))
     own_head.wait()
@@ -256,12 +243,12 @@
     z_copy(1, True, 1).start()
     z_copy(1, False, 1).start()
     on_c(0)
-    multiply(0, 0)
+    multiply((0, 1, 0, 0), (0, 1, 0, 1))
     on_y(0, 0)
     on_hz(0)
     on_y(0, 1)
     on_c(1)
-    multiply(1, 0)
+    multiply((1, 1, 0, 0), (1, 1, 0, 1))
     on_hz(1)
     on_hy(0)
     on_hz(2)
@@ -272,36 +259,31 @@
     on_z(0, 1)
     on_hy(3)
     on_c(2)
-    multiply(2, 0)
+    multiply((2, 1, 0, 0), (2, 1, 0, 1))
     on_y(1, 0)
     on_z(1, 0)
     on_y(1, 1)
     on_z(1, 1)
     on_c(3)
-    multiply(3, 0)
     on_c(4)
-    multiply(4, 0)
+    multiply((3, 1, 0, 0), (3, 1, 0, 1), (4, 1, 0, 0), (4, 1, 0, 1))
     on_y(2, 0)
     on_z(2, 0)
+    on_hend(0)
+    multiply((0, 1, 1, own_tile), (1, 1, 1, own_tile), (2, 1, 1, own_tile), (3, 1, 1, own_tile))
     on_y(2, 1)
     on_z(2, 1)
+    multiply((4, 1, 1, own_tile))
     on_c(5)
-    multiply(5, 0)
     on_c(6)
-    multiply(6, 0)
+    multiply((5, 1, 0, 0), (5, 1, 0, 1), (6, 1, 0, 0), (6, 1, 0, 1))
     on_y(3, 0)
-    on_hend(0, 4)
-    multiply(0, 1)
-    multiply(1, 1)
-    multiply(2, 1)
-    multiply(3, 1)
-    on_y(3, 1)
-    multiply(4, 1)
-    multiply(5, 1)
-    multiply(6, 1)
+    on_z(3, 1)
+    multiply((5, 1, 1, own_tile), (6, 1, 1, own_tile))
+    on_hend(1)
+    multiply((0, 1, 1, far_tile), (1, 1, 1, far_tile), (2, 1, 1, far_tile), (3, 1, 1, far_tile), (4, 1, 1, far_tile), (5, 1, 1, far_tile), (6, 1, 1, far_tile))
     on_c(7)
-    multiply(7, 0)
-    multiply(7, 1)
+    multiply((7, 1, 0, 0), (7, 1, 0, 1), (7, 1, 1, own_tile), (7, 1, 1, far_tile))
 
     lane = lax.broadcasted_iota(jnp.int32, (8, 128), 1)
     line = lax.broadcasted_iota(jnp.int32, (8, 128), 0)
@@ -411,12 +393,13 @@
     out_ref[...] = placed[0:4, 0:16]
 
     for side in range(2):
-        for k in range(3):
-            for n in range(CUTS):
+        for k in range(4):
+            for n in VIA_Z if k == 3 else range(CUTS):
                 z_copy(k, side == 0, n).wait_send()
         for m in range(4):
             for n in range(CUTS):
-                y_copy(m, side == 0, n).wait_send()
+                if m < 3 or n not in VIA_Z:
+                    y_copy(m, side == 0, n).wait_send()
         for g in range(8):
             for n in range(CUTS):
                 c_copy(g, side, n).wait_send()
@@ -444,7 +427,7 @@
             pltpu.SMEM((32,), jnp.int32),
             pltpu.VMEM((2, 512, width), jnp.bfloat16),
             pltpu.VMEM((32, HALF, width), jnp.bfloat16),
-            pltpu.VMEM((2, 4 * HALF, NT), jnp.float32),
+            pltpu.VMEM((4, 8 * HALF, NT), jnp.float32),
             pltpu.VMEM((2, 8, 512), jnp.float32),
             pltpu.VMEM((2, 8, 512), jnp.float32),
             pltpu.VMEM((2, 8, 512), jnp.float32),
@@ -453,7 +436,7 @@
             pltpu.VMEM((8, 2, 1, 128), jnp.float32),
             pltpu.VMEM((3, 1, 128), jnp.float32),
             pltpu.VMEM((32, 3, 1, 128), jnp.float32),
-            dma((4,)), dma((2, 3, CUTS)), dma((2, 3, CUTS)), dma((2, 4, CUTS)), dma((2, 4, CUTS)),
+            dma((4,)), dma((2, 4, CUTS)), dma((2, 4, CUTS)), dma((2, 4, CUTS)), dma((2, 4, CUTS)),
             dma((2, 8, CUTS)), dma((2, 8, CUTS)),
             dma((PARTS,)), dma((PARTS,)), dma((PARTS,)), dma((PARTS,)),
             dma((2, PARTS, 3)), dma((2, PARTS, 3)), dma((2,)), dma((2,)),

time: 65.2 us -> 63.4 us (0.972)
  Pallas kernels: 63.8 us -> 62.1 us
    pallas_call x1, Pallas kernels: 63.8 us -> 62.1 us  [per_device(): pl.pallas_call(kernel, out_shape=jax.ShapeDtypeStruct((4, 16), jnp.float3...]
where the time goes in v3:
time: 63.4 us; the launch traced here: 63.3 us
  Pallas kernels  62.1 us (98%)
  local copies, waits for them, and re-layouts  1.26 us (2%)
    pallas_call x1, Pallas kernels, per_device(): pl.pallas_call(kernel, out_shape=jax.ShapeDtypeStruct((4, 16), jnp.float3...  62.1 us

profile of v3, /device:TPU:1, one launch (start us, length us, event | category | flops | bytes accessed | tf_op | source)
XLA Modules:
  0.0 63.3 jit_solution(4246045665495797984)
XLA Ops:
  0.0 62.1 %score_kernel.1 = f32[4,16]{1,0:T(4,128)} custom-call(bf16[512,2048]{1,0:T(8,128)(2,1)} %bitcast.3, bf16[2,64,2048]{2,1,0:T(8,128)(2,1)} %bitcast.4, s32[1,128]{1,0:T(1,128)} %bitcast.5, s32[4,4]{1,0:T(4,128)} %member_hbm.1), custom_call_target="tpu_custom_call" | custom-call | tf_op jit(solution)/shard_map/score_kernel/pallas_call | solution.py:419
  62.1 1.3 %copy.6 = f32[4,16]{1,0:T(4,128)} copy(f32[4,16]{1,0:T(4,128)} %score_kernel.1) | data formatting | bytes 512

commit v4 on v3

--- a/solution.py
+++ b/solution.py
@@ -130,12 +130,16 @@
         )
 
     def hx_copy(part, i, dx):
-        share = ((y_hi + part) % 2) * 4 + x
+        to_x, owner = dx, x
+        if part == 1 and dx == 2:
+            to_x = 1 if i % 2 == 0 else 3
+            owner = (x + 4 - to_x) % 4
+        share = ((y_hi + part) % 2) * 4 + owner
         rows = pl.ds(pl.multiple_of(share * 64 + i * ROWS, ROWS), ROWS)
         return pltpu.make_async_remote_copy(
             src_ref=hid.at[1, rows, :], dst_ref=hid.at[1, rows, :],
             send_sem=hx_send.at[part, i, dx - 1], recv_sem=hx_recv.at[part, i, dx - 1],
-            device_id=device(0, 0, dx, 0), device_id_type=MESH,
+            device_id=device(0, 0, to_x, 0), device_id_type=MESH,
         )
 
     def columns(tile):
@@ -213,12 +217,18 @@
 
     def on_hy(i):
         hy_copy(i).wait_recv()
-        for dx in FIRST_X:
+        for dx in (1, 3):
             hx_copy(1, i, dx).start()
+
+    def on_hx(i):
+        for dx in (1, 3):
+            hx_copy(1, i, dx).wait_recv()
+            if (dx == 1) == (i % 2 == 0):
+                hx_copy(1, i, 2).start()
 
     def on_hend(part):
         for i in range(PARTS):
-            for dx in (1, 3, 2):
+            for dx in (1, 3, 2) if part == 0 else (2,):
                 hx_copy(part, i, dx).wait_recv()
 
     pl.semaphore_wait(barrier, len(near))
@@ -250,10 +260,10 @@
     on_c(1)
     multiply((1, 1, 0, 0), (1, 1, 0, 1))
     on_hz(1)
+    on_hz(2)
+    on_hz(3)
     on_hy(0)
-    on_hz(2)
     on_hy(1)
-    on_hz(3)
     on_z(0, 0)
     on_hy(2)
     on_z(0, 1)
@@ -262,26 +272,30 @@
     multiply((2, 1, 0, 0), (2, 1, 0, 1))
     on_y(1, 0)
     on_z(1, 0)
+    on_hx(0)
+    on_hx(1)
+    on_hend(0)
+    multiply((0, 1, 1, own_tile), (1, 1, 1, own_tile))
     on_y(1, 1)
     on_z(1, 1)
+    on_hx(2)
+    on_hx(3)
     on_c(3)
-    on_c(4)
-    multiply((3, 1, 0, 0), (3, 1, 0, 1), (4, 1, 0, 0), (4, 1, 0, 1))
+    multiply((2, 1, 1, own_tile), (3, 1, 0, 0), (3, 1, 0, 1), (3, 1, 1, own_tile))
     on_y(2, 0)
     on_z(2, 0)
-    on_hend(0)
-    multiply((0, 1, 1, own_tile), (1, 1, 1, own_tile), (2, 1, 1, own_tile), (3, 1, 1, own_tile))
+    on_c(4)
+    multiply((4, 1, 0, 0), (4, 1, 0, 1), (4, 1, 1, own_tile))
     on_y(2, 1)
     on_z(2, 1)
-    multiply((4, 1, 1, own_tile))
+    on_hend(1)
+    multiply((0, 1, 1, far_tile), (1, 1, 1, far_tile), (2, 1, 1, far_tile))
     on_c(5)
-    on_c(6)
-    multiply((5, 1, 0, 0), (5, 1, 0, 1), (6, 1, 0, 0), (6, 1, 0, 1))
+    multiply((5, 1, 0, 0), (5, 1, 0, 1), (5, 1, 1, own_tile), (5, 1, 1, far_tile))
     on_y(3, 0)
     on_z(3, 1)
-    multiply((5, 1, 1, own_tile), (6, 1, 1, own_tile))
-    on_hend(1)
-    multiply((0, 1, 1, far_tile), (1, 1, 1, far_tile), (2, 1, 1, far_tile), (3, 1, 1, far_tile), (4, 1, 1, far_tile), (5, 1, 1, far_tile), (6, 1, 1, far_tile))
+    on_c(6)
+    multiply((6, 1, 0, 0), (6, 1, 0, 1), (6, 1, 1, own_tile), (6, 1, 1, far_tile), (3, 1, 1, far_tile), (4, 1, 1, far_tile))
     on_c(7)
     multiply((7, 1, 0, 0), (7, 1, 0, 1), (7, 1, 1, own_tile), (7, 1, 1, far_tile))
 
@@ -313,16 +327,16 @@
         msg[r, 0] = lse_tile[r:r + 1, :]
         msg[r, 1] = target_tile[r:r + 1, :]
 
-    def to_plane(k, _):
+    def to_plane(k):
         to = (vocab + k) % 8
         pltpu.make_async_remote_copy(
             src_ref=msg.at[to], dst_ref=got1.at[7 - k],
             send_sem=tail_send.at[0], recv_sem=tail_recv.at[0],
             device_id=(shadow, to), device_id_type=MESH,
         ).start()
-        return 0
-
-    lax.fori_loop(1, 8, to_plane, 0)
+
+    for k in (6, 2, 5, 7, 4, 1, 3):
+        to_plane(k)
     got1[7] = msg[vocab]
     all_plane = pltpu.make_async_remote_copy(
         src_ref=msg.at[0:7], dst_ref=got1.at[0:7],
@@ -343,7 +357,7 @@
     msg2[0] = top + jnp.log(jnp.sum(jnp.exp(pieces - top[None]), axis=0))
     msg2[1] = jnp.sum(got1[:, 1], axis=0)
 
-    def to_shadows(k, _):
+    def to_shadows(k):
         dz, dy, dcore = k // 4, (k // 2) % 2, k % 2
         to = (((z + dz) % NZ) * 2 + (y_lo + dy) % 2) * 2 + (core + dcore) % 2
         pltpu.make_async_remote_copy(
@@ -351,9 +365,10 @@
             send_sem=tail_send.at[1], recv_sem=tail_recv.at[1],
             device_id=(to, vocab), device_id_type=MESH,
         ).start()
-        return 0
-
-    lax.fori_loop(1, 32, to_shadows, 0)
+
+    for dz in (4, 3, 5, 2, 6, 1, 7, 0):
+        for k in range(max(4 * dz, 1), 4 * dz + 4):
+            to_shadows(k)
     got2[0] = msg2[...]
     all_shadows = pltpu.make_async_remote_copy(
         src_ref=got2.at[1:32], dst_ref=got2.at[1:32],

time: 63.4 us -> 63.1 us (level)
  no operation moved by 1% of the time
where the time goes in v4:
time: 63.1 us; the launch traced here: 63 us
  Pallas kernels  61.7 us (98%)
  local copies, waits for them, and re-layouts  1.26 us (2%)
    pallas_call x1, Pallas kernels, per_device(): pl.pallas_call(kernel, out_shape=jax.ShapeDtypeStruct((4, 16), jnp.float3...  61.7 us

profile of v4, /device:TPU:1, one launch (start us, length us, event | category | flops | bytes accessed | tf_op | source)
XLA Modules:
  0.0 63.0 jit_solution(15344565985327538752)
XLA Ops:
  0.0 61.7 %score_kernel.1 = f32[4,16]{1,0:T(4,128)} custom-call(bf16[512,2048]{1,0:T(8,128)(2,1)} %bitcast.3, bf16[2,64,2048]{2,1,0:T(8,128)(2,1)} %bitcast.4, s32[1,128]{1,0:T(1,128)} %bitcast.5, s32[4,4]{1,0:T(4,128)} %member_hbm.1), custom_call_target="tpu_custom_call" | custom-call | tf_op jit(solution)/shard_map/score_kernel/pallas_call | solution.py:434
  61.7 1.3 %copy.6 = f32[4,16]{1,0:T(4,128)} copy(f32[4,16]{1,0:T(4,128)} %score_kernel.1) | data formatting | bytes 512

commit v5 on v4

--- a/solution.py
+++ b/solution.py
@@ -433,7 +433,7 @@
     dma = pltpu.SemaphoreType.DMA
     return pl.pallas_call(
         kernel,
-        out_shape=jax.ShapeDtypeStruct((4, 16), jnp.float32),
+        out_shape=pltpu.VMEM((4, 16), jnp.float32),
         in_specs=[pl.BlockSpec(memory_space=pltpu.HBM)] * 4,
         out_specs=pl.BlockSpec(memory_space=pltpu.VMEM),
         scratch_shapes=[
@@ -457,14 +457,14 @@
             dma((2, PARTS, 3)), dma((2, PARTS, 3)), dma((2,)), dma((2,)),
         ],
         compiler_params=pltpu.CompilerParams(
-            collective_id=0, has_side_effects=True, vmem_limit_bytes=67043328
+            collective_id=0, has_side_effects=True, vmem_limit_bytes=60 * 2**20
         ),
         name="score_kernel",
-    )(
+    )(*(pltpu.with_memory_space_constraint(a, pltpu.HBM) for a in (
         hidden.reshape(shadow_count * token_count, width),
         unembedding.reshape(2, HALF, width),
         targets.reshape(1, token_count), membership,
-    )
+    )))
 
 
 def solution(mesh):

time: 63.1 us -> 61.8 us (0.979)
  local copies, waits for them, and re-layouts: 1.26 us -> 0.58 us
    unnamed x1, local copies, waits for them, and re-layouts: 1.26 us -> 0.58 us
where the time goes in v5:
time: 61.8 us; the launch traced here: 61.7 us
  Pallas kernels  61.1 us (99%)
    pallas_call x1, Pallas kernels, per_device(): pl.pallas_call(kernel, out_shape=pltpu.VMEM((4, 16), jnp.float32), in_spe...  61.1 us

profile of v5, /device:TPU:1, one launch (start us, length us, event | category | flops | bytes accessed | tf_op | source)
XLA Modules:
  0.0 61.7 jit_solution(881003825608099344)
XLA Ops:
  0.0 61.1 %score_kernel.1 = f32[4,16]{1,0:T(4,128)S(1)} custom-call(bf16[512,2048]{1,0:T(8,128)(2,1)} %bitcast.3, bf16[2,64,2048]{2,1,0:T(8,128)(2,1)} %bitcast.4, s32[1,128]{1,0:T(1,128)} %bitcast.5, s32[4,4]{1,0:T(4,128)} %member_hbm.1), custom_call_target="tpu_custom_call" | custom-call | tf_op jit(solution)/shard_map/score_kernel/pallas_call | solution.py:434
  61.1 0.6 copy.6

commit v6 on v5

--- a/solution.py
+++ b/solution.py
@@ -55,6 +55,11 @@
             (to_y // 2) * 4 + (x + dx) % 4,
         )
 
+    barrier = pltpu.get_barrier_semaphore()
+    near = ((4, 0, 0, 0), (1, 0, 0, 0), (7, 0, 0, 0), (0, 1, 0, 0), (0, 3, 0, 0), (0, 2, 0, 0), (0, 0, 1, 0), (0, 0, 3, 0), (0, 0, 2, 0), (0, 0, 0, 1))
+    for offset in near:
+        pl.semaphore_signal(barrier, inc=1, device_id=device(*offset), device_id_type=MESH)
+
     own_head = pltpu.make_async_copy(head_hbm, head.at[pl.ds(0, 2)], local_sem.at[0])
     own_hid = pltpu.make_async_copy(hidden_hbm, hid.at[0], local_sem.at[1])
     own_tg = pltpu.make_async_copy(targets_hbm, targets_ref, local_sem.at[2])
@@ -63,11 +68,6 @@
     own_hid.start()
     own_tg.start()
     own_member.start()
-
-    barrier = pltpu.get_barrier_semaphore()
-    near = ((1, 0, 0, 0), (7, 0, 0, 0), (4, 0, 0, 0), (0, 1, 0, 0), (0, 3, 0, 0), (0, 2, 0, 0), (0, 0, 1, 0), (0, 0, 3, 0), (0, 0, 2, 0), (0, 0, 0, 1))
-    for offset in near:
-        pl.semaphore_signal(barrier, inc=1, device_id=device(*offset), device_id_type=MESH)
 
     high[...] = jnp.full_like(high, NEG_FILL)
     total[...] = jnp.zeros_like(total)
@@ -233,12 +233,6 @@
 
     pl.semaphore_wait(barrier, len(near))
     own_head.wait()
-    for n in range(CUTS):
-        c_copy(0, 0, n).start()
-        c_copy(0, 1, n).start()
-    for n in range(CUTS):
-        y_copy(0, True, n).start()
-        y_copy(0, False, n).start()
     own_hid.wait()
     hz_copy(0).start()
     hz_copy(1).start()
@@ -252,6 +246,12 @@
     z_copy(1, False, 0).start()
     z_copy(1, True, 1).start()
     z_copy(1, False, 1).start()
+    for n in range(CUTS):
+        c_copy(0, 0, n).start()
+        c_copy(0, 1, n).start()
+    for n in range(CUTS):
+        y_copy(0, True, n).start()
+        y_copy(0, False, n).start()
     on_c(0)
     multiply((0, 1, 0, 0), (0, 1, 0, 1))
     on_y(0, 0)

time: 61.8 us -> 61.8 us (level)
  no operation moved by 1% of the time
where the time goes in v6:
time: 61.8 us; the launch traced here: 61.7 us
  Pallas kernels  61.1 us (99%)
    pallas_call x1, Pallas kernels, per_device(): pl.pallas_call(kernel, out_shape=pltpu.VMEM((4, 16), jnp.float32), in_spe...  61.1 us

profile of v6, /device:TPU:1, one launch (start us, length us, event | category | flops | bytes accessed | tf_op | source)
XLA Modules:
  0.0 61.7 jit_solution(7505167091481093104)
XLA Ops:
  0.0 61.1 %score_kernel.1 = f32[4,16]{1,0:T(4,128)S(1)} custom-call(bf16[512,2048]{1,0:T(8,128)(2,1)} %bitcast.3, bf16[2,64,2048]{2,1,0:T(8,128)(2,1)} %bitcast.4, s32[1,128]{1,0:T(1,128)} %bitcast.5, s32[4,4]{1,0:T(4,128)} %member_hbm.1), custom_call_target="tpu_custom_call" | custom-call | tf_op jit(solution)/shard_map/score_kernel/pallas_call | solution.py:434
  61.1 0.6 copy.6

commit v7 on v5

--- a/solution.py
+++ b/solution.py
@@ -286,16 +286,17 @@
     on_z(2, 0)
     on_c(4)
     multiply((4, 1, 0, 0), (4, 1, 0, 1), (4, 1, 1, own_tile))
+    on_hend(1)
+    multiply((0, 1, 1, far_tile))
     on_y(2, 1)
     on_z(2, 1)
-    on_hend(1)
-    multiply((0, 1, 1, far_tile), (1, 1, 1, far_tile), (2, 1, 1, far_tile))
+    multiply((1, 1, 1, far_tile), (2, 1, 1, far_tile), (3, 1, 1, far_tile), (4, 1, 1, far_tile))
     on_c(5)
     multiply((5, 1, 0, 0), (5, 1, 0, 1), (5, 1, 1, own_tile), (5, 1, 1, far_tile))
     on_y(3, 0)
     on_z(3, 1)
     on_c(6)
-    multiply((6, 1, 0, 0), (6, 1, 0, 1), (6, 1, 1, own_tile), (6, 1, 1, far_tile), (3, 1, 1, far_tile), (4, 1, 1, far_tile))
+    multiply((6, 1, 0, 0), (6, 1, 0, 1), (6, 1, 1, own_tile), (6, 1, 1, far_tile))
     on_c(7)
     multiply((7, 1, 0, 0), (7, 1, 0, 1), (7, 1, 1, own_tile), (7, 1, 1, far_tile))
 

time: 61.8 us -> 62 us (level)
  no operation moved by 1% of the time
where the time goes in v7:
time: 62 us; the launch traced here: 61.9 us
  Pallas kernels  61.4 us (99%)
    pallas_call x1, Pallas kernels, per_device(): pl.pallas_call(kernel, out_shape=pltpu.VMEM((4, 16), jnp.float32), in_spe...  61.4 us

profile of v7, /device:TPU:1, one launch (start us, length us, event | category | flops | bytes accessed | tf_op | source)
XLA Modules:
  0.0 61.9 jit_solution(6002451551615506489)
XLA Ops:
  0.0 61.4 %score_kernel.1 = f32[4,16]{1,0:T(4,128)S(1)} custom-call(bf16[512,2048]{1,0:T(8,128)(2,1)} %bitcast.3, bf16[2,64,2048]{2,1,0:T(8,128)(2,1)} %bitcast.4, s32[1,128]{1,0:T(1,128)} %bitcast.5, s32[4,4]{1,0:T(4,128)} %member_hbm.1), custom_call_target="tpu_custom_call" | custom-call | tf_op jit(solution)/shard_map/score_kernel/pallas_call | solution.py:435
  61.4 0.6 copy.6
